TPU v7x, 32 devices: a whole 2x2x4 slice. The times are simulated.
32 devices in a mesh: kx: 2 (over x), ky: 4 (over y, core), kz: 4 (over z).
Axes of the slice: x: 2, y: 2, z: 4, core: 2. Of those that a mesh axis runs over, the one named last changes fastest.
Arguments:
- coefficients: bfloat16 [2, 2, 4, 4, 512, 2048], P(None, 'kx', 'ky', 'kz'), may hold values from -1 to 1
- shift_blocks: int32 [3], replicated, may hold values from 1 to 15, as said below
Outputs:
- centre: float32 [3, 512], replicated
- spread: float32 [3, 512], replicated
- coherence: float32 [3, 2, 4, 4], P(None, 'kx', 'ky', 'kz')
Inputs may be any that keep to these rules, and one draw needn't show every extreme that they name: The coefficients one period further along direction d are those of the first k-point of the string with plane-wave index g read at (g + 128 * shift_blocks[d]) mod 2048.
All inputs are finite; a program needn't handle non-finite values.
Results may differ from a plain program's by a relative error of at most 0.0003.
Values may be sent and summed in bfloat16 or wider, within the bound.
A program may use at most 128 MiB of HBM per device.

v0:
```python
import functools

import jax
import jax.numpy as jnp
from jax import lax
from jax.experimental import pallas as pl
from jax.experimental.pallas import tpu as pltpu
from jax.sharding import PartitionSpec as P

MESH = pl.DeviceIdType.MESH
AXES = ("kx", "ky", "kz")
LANES = 128
ROWS = 256
STRIP = 32


def greeted(count):
    return range(1, count) if count > 4 else sorted({1, count - 1})


def merged(parts, count):
    mean = functools.reduce(jnp.add, [part[0] for part in parts]) / len(parts)
    square = functools.reduce(jnp.add, [part[1] for part in parts])
    apart = functools.reduce(jnp.add, [(part[0] - mean) * (part[0] - mean) for part in parts])
    return mean, square + count * apart


def kernel(sizes, shift_ref, a_ref, sums_ref,
           own, partner, rolled, diag_re, diag_im, total, stats, heard,
           own_sem, send_sem, recv_sem, stat_send, stat_recv):
    planes, bands, width = own.shape[1:]
    chunks, cut = partner.shape[1], partner.shape[3]
    tiles, row_tiles = width // LANES, bands // ROWS
    place = [lax.axis_index(axis) for axis in AXES]
    points = [(d, p) for d in range(3) for p in range(planes)]

    def beside(d, step):
        return {AXES[d]: lax.rem(place[d] + step, sizes[d])}

    load = pltpu.make_async_copy(a_ref, own, own_sem)
    load.start()
    barrier = pltpu.get_barrier_semaphore()
    greetings = 0
    for d in range(3):
        for step in greeted(sizes[d]):
            pl.semaphore_signal(barrier, inc=1, device_id=beside(d, step), device_id_type=MESH)
            greetings += 1
    pl.semaphore_wait(barrier, greetings)

    def copy_of(i, c):
        d, p = points[i]
        source = (p + 1) % planes if d == 0 else p
        return pltpu.make_async_remote_copy(
            src_ref=a_ref.at[:, source, pl.ds(pl.multiple_of(c * cut, cut), cut), :],
            dst_ref=partner.at[i, c],
            send_sem=send_sem.at[i, c],
            recv_sem=recv_sem.at[i, c],
            device_id=beside(d, sizes[d] - 1),
            device_id_type=MESH,
        )

    def inner_copy(i, c):
        p = points[i][1]
        return pltpu.make_async_copy(
            a_ref.at[:, p + 1, pl.ds(pl.multiple_of(c * cut, cut), cut), :], partner.at[i, c], recv_sem.at[i, c]
        )

    def inner(i):
        d, p = points[i]
        return d == 0 and p < planes - 1

    def launch(c, carry):
        for i in range(len(points)):
            (inner_copy(i, c) if inner(i) else copy_of(i, c)).start()
        return carry

    lax.fori_loop(0, chunks, launch, 0)

    total[...] = jnp.zeros_like(total)
    diag_re[...] = jnp.zeros_like(diag_re)
    diag_im[...] = jnp.zeros_like(diag_im)
    load.wait()
    for i, (d, p) in enumerate(points):
        wraps = place[d] == sizes[d] - 1
        shift = 0 if inner(i) else jnp.where(wraps, shift_ref[d], 0)

        moves = [] if inner(i) else [(LANES << bit, (shift >> bit) & 1 == 1) for bit in range((tiles - 1).bit_length())]

        def turn(block, carry, i=i, p=p, moves=moves):
            rows = pl.ds(pl.multiple_of(block * STRIP, STRIP), STRIP)
            for part in range(2):
                value = own[part, p, rows, :]
                for amount, taken in moves:
                    moved = jnp.concatenate([value[:, width - amount:], value[:, :width - amount]], axis=1)
                    value = jnp.where(taken, moved, value)
                rolled[i, part, rows, :] = value
            return carry

        lax.fori_loop(0, bands // STRIP, turn, 0)

    row = lax.broadcasted_iota(jnp.int32, (ROWS, cut), 0)
    column = lax.broadcasted_iota(jnp.int32, (ROWS, cut), 1)

    def arrived(i, c):
        (inner_copy(i, c).wait if inner(i) else copy_of(i, c).wait_recv)()

    def measure(i, c, start, rows):
        left = rolled[i, :, pl.ds(pl.multiple_of(start, rows), rows), :].reshape(2 * rows, width)
        right = partner[i, c].reshape(2 * cut, width)
        product = lax.dot_general(left, right, (((1,), (1,)), ((), ())), preferred_element_type=jnp.float32)
        re = product[:rows, :cut] + product[rows:, cut:]
        im = product[:rows, cut:] - product[rows:, :cut]
        squares = re * re + im * im
        total[i] += jnp.sum(squares.reshape(rows // 8, 8, cut), axis=0)
        same = row[:rows] + start == column[:rows] + c * cut
        diag_re[i, pl.ds(c, 1), :] += jnp.sum(jnp.where(same, re, 0.0), axis=0, keepdims=True)
        diag_im[i, pl.ds(c, 1), :] += jnp.sum(jnp.where(same, im, 0.0), axis=0, keepdims=True)

    def whole(i, c):
        def one(r, carry):
            measure(i, c, r * ROWS, ROWS)
            return carry
        lax.fori_loop(0, row_tiles, one, 0)

    order = [i for d in (1, 0, 2) for i, point in enumerate(points) if point[0] == d]

    def chunk(c, carry):
        for i in order:
            arrived(i, c)
            whole(i, c)
        return carry

    lax.fori_loop(0, chunks - 1, chunk, 0)
    last = chunks - 1
    edge = bands - cut
    for i in order:
        arrived(i, last)
        if points[i][0] == 1:
            whole(i, last)
        else:
            measure(i, last, edge, cut)
    phases = jnp.arctan2(diag_im[...], diag_re[...])
    groups = phases.reshape(3, planes, chunks, cut)
    mean, square = merged([(groups[:, p], jnp.zeros_like(groups[:, p])) for p in range(planes)], 1.0)
    count = float(planes)

    def stat_copy(d, step):
        return pltpu.make_async_remote_copy(
            src_ref=stats.at[d],
            dst_ref=heard[d].at[step - 1],
            send_sem=stat_send[d].at[step - 1],
            recv_sem=stat_recv[d].at[step - 1],
            device_id=beside(d, step),
            device_id_type=MESH,
        )

    for d in range(3):
        stats[d, 0] = mean
        stats[d, 1] = square
        for step in range(1, sizes[d]):
            stat_copy(d, step).start()
        if d == 0:
            for i in order:
                if points[i][0] != 1:
                    for start in range(0, edge, ROWS):
                        measure(i, last, start, min(ROWS, edge - start))
        for step in range(1, sizes[d]):
            stat_copy(d, step).wait_recv()
        members = [(mean, square)] + [(heard[d][step - 1, 0], heard[d][step - 1, 1]) for step in range(1, sizes[d])]
        ordered = []
        for slot in range(sizes[d]):
            entry = None
            for step in range(sizes[d]):
                owner = lax.rem(place[d] - step + sizes[d], sizes[d])
                if entry is None:
                    entry = members[step]
                else:
                    entry = tuple(jnp.where(owner == slot, new, old) for new, old in zip(members[step], entry))
            ordered.append(entry)
        mean, square = merged(ordered, count)
        count *= sizes[d]

    for d in range(3):
        sums_ref[d * chunks:(d + 1) * chunks, :] = mean[d]
        sums_ref[(3 + d) * chunks:(4 + d) * chunks, :] = square[d]
    for i in range(len(points)):
        sums_ref[6 * chunks + 8 * i:6 * chunks + 8 * (i + 1), :] = total[i]

    for d in range(3):
        for step in range(1, sizes[d]):
            stat_copy(d, step).wait_send()

    def sent(c, carry):
        for i in range(len(points)):
            if not inner(i):
                copy_of(i, c).wait_send()
        return carry

    lax.fori_loop(0, chunks, sent, 0)


def results(sizes, planes, sums_ref, centre_ref, spread_ref, coherence_ref):
    bands = centre_ref.shape[1]
    chunks, count = bands // LANES, planes * sizes[0] * sizes[1] * sizes[2]
    lengths = (planes * sizes[0], sizes[1], sizes[2])
    for d in range(3):
        scale = lengths[d] / (2.0 * jnp.pi)
        for c in range(chunks):
            lanes = slice(c * LANES, (c + 1) * LANES)
            centre_ref[d:d + 1, lanes] = -scale * sums_ref[d * chunks + c:d * chunks + c + 1, :]
            at = (3 + d) * chunks + c
            spread_ref[d:d + 1, lanes] = scale * scale * (sums_ref[at:at + 1, :] / count)
    for i in range(3 * planes):
        at = 6 * chunks + 8 * i
        coherence_ref[i] = jnp.sum(sums_ref[at:at + 8, :]) / bands


def solution(mesh):
    sizes = tuple(mesh.shape[axis] for axis in AXES)

    def shards(coefficients, shift_blocks):
        planes, bands, width = coefficients.shape[1], coefficients.shape[4], coefficients.shape[5]
        own_planes = coefficients.reshape(2, planes, bands, width)
        chunks = bands // LANES
        pairs = 3 * planes
        vmem = pl.BlockSpec(memory_space=pltpu.VMEM)
        sums = pl.pallas_call(
            functools.partial(kernel, sizes),
            out_shape=jax.ShapeDtypeStruct((6 * chunks + 8 * pairs, LANES), jnp.float32),
            in_specs=[pl.BlockSpec(memory_space=pltpu.SMEM), pl.BlockSpec(memory_space=pl.ANY)],
            out_specs=vmem,
            scratch_shapes=[
                pltpu.VMEM((2, planes, bands, width), jnp.bfloat16),
                pltpu.VMEM((pairs, chunks, 2, LANES, width), jnp.bfloat16),
                pltpu.VMEM((pairs, 2, bands, width), jnp.bfloat16),
                pltpu.VMEM((pairs, chunks, LANES), jnp.float32),
                pltpu.VMEM((pairs, chunks, LANES), jnp.float32),
                pltpu.VMEM((pairs, 8, LANES), jnp.float32),
                pltpu.VMEM((3, 2, 3, chunks, LANES), jnp.float32),
                [pltpu.VMEM((size - 1, 2, 3, chunks, LANES), jnp.float32) for size in sizes],
                pltpu.SemaphoreType.DMA,
                pltpu.SemaphoreType.DMA((pairs, chunks)),
                pltpu.SemaphoreType.DMA((pairs, chunks)),
                [pltpu.SemaphoreType.DMA((size - 1,)) for size in sizes],
                [pltpu.SemaphoreType.DMA((size - 1,)) for size in sizes],
            ],
            compiler_params=pltpu.CompilerParams(
                collective_id=0, has_side_effects=True, vmem_limit_bytes=60 * 1024 * 1024
            ),
        )(shift_blocks, own_planes)
        centre, spread, coherence = pl.pallas_call(
            functools.partial(results, sizes, planes),
            out_shape=(
                jax.ShapeDtypeStruct((3, bands), jnp.float32),
                jax.ShapeDtypeStruct((3, bands), jnp.float32),
                jax.ShapeDtypeStruct((pairs,), jnp.float32),
            ),
            in_specs=[vmem],
            out_specs=(vmem, vmem, pl.BlockSpec(memory_space=pltpu.SMEM)),
        )(sums)
        return centre, spread, coherence.reshape(3, planes, 1, 1)

    in_specs = (P(None, "kx", "ky", "kz", None, None), P())
    out_specs = (P(), P(), P(None, "kx", "ky", "kz"))
    return jax.shard_map(shards, mesh=mesh, in_specs=in_specs, out_specs=out_specs, check_vma=False)
```

profile of v0, /device:TPU:0, one launch (start us, length us, event | category | flops | bytes accessed | tf_op | source)
XLA Modules:
  0.0 112.0 jit_solution(1798436498701465980)
XLA Ops:
  0.6 110.0 %shard_map.49.sums_ref = f32[48,128]{1,0:T(8,128)} custom-call(s32[3]{0:T(128)} %shift_ref.1, bf16[2,1,512,2048]{3,2,1,0:T(8,128)(2,1)} %bitcast.2), custom_call_target="tpu_custom_call" | custom-call | tf_op jit(solution)/shard_map/pallas_call | solution.py:227
  110.7 1.4 %shard_map.50 = (f32[3,512]{1,0:T(4,128)}, f32[3,512]{1,0:T(4,128)}, f32[3]{0:T(128)}) custom-call(f32[48,128]{1,0:T(8,128)} %shard_map.49.sums_ref), custom_call_target="tpu_custom_call" | custom-call | tf_op jit(solution)/shard_map/pallas_call | solution.py:251
where the time goes:
time: 112 us
  Pallas kernels  111 us (99%)
    pallas_call x1, Pallas kernels, shards(): pl.pallas_call(functools.partial(kernel, sizes), out_shape=jax.ShapeDtype...  110 us

commit v1 on v0

--- a/solution.py
+++ b/solution.py
@@ -226,7 +226,7 @@
         vmem = pl.BlockSpec(memory_space=pltpu.VMEM)
         sums = pl.pallas_call(
             functools.partial(kernel, sizes),
-            out_shape=jax.ShapeDtypeStruct((6 * chunks + 8 * pairs, LANES), jnp.float32),
+            out_shape=pltpu.VMEM((6 * chunks + 8 * pairs, LANES), jnp.float32),
             in_specs=[pl.BlockSpec(memory_space=pltpu.SMEM), pl.BlockSpec(memory_space=pl.ANY)],
             out_specs=vmem,
             scratch_shapes=[
@@ -248,6 +248,7 @@
                 collective_id=0, has_side_effects=True, vmem_limit_bytes=60 * 1024 * 1024
             ),
         )(shift_blocks, own_planes)
+        sums = pltpu.with_memory_space_constraint(sums, pltpu.VMEM)
         centre, spread, coherence = pl.pallas_call(
             functools.partial(results, sizes, planes),
             out_shape=(

time: 112 us -> 111 us (level)
  no operation moved by 1% of the time
where the time goes in v1:
time: 111 us
  Pallas kernels  110 us (99%)
    pallas_call x1, Pallas kernels, shards(): pl.pallas_call(functools.partial(kernel, sizes), out_shape=pltpu.VMEM((6...  109 us

profile of v1, /device:TPU:0, one launch (start us, length us, event | category | flops | bytes accessed | tf_op | source)
XLA Modules:
  0.0 110.7 jit_solution(8281612803145327456)
XLA Ops:
  0.6 109.4 %shard_map.49.sums_ref = f32[48,128]{1,0:T(8,128)S(1)} custom-call(s32[3]{0:T(128)} %shift_ref.1, bf16[2,1,512,2048]{3,2,1,0:T(8,128)(2,1)} %bitcast.2), custom_call_target="tpu_custom_call" | custom-call | tf_op jit(solution)/shard_map/pallas_call | solution.py:227
  110.1 0.6 shard_map.50

commit v2 on v1

v2 whole, which is shorter than its diff:
```python
import functools

import jax
import jax.numpy as jnp
from jax import lax
from jax.experimental import pallas as pl
from jax.experimental.pallas import tpu as pltpu
from jax.sharding import PartitionSpec as P

MESH = pl.DeviceIdType.MESH
AXES = ("kx", "ky", "kz")
LANES = 128
ROWS = 256
STRIP = 32


def added(parts):
    return functools.reduce(jnp.add, parts)


class Plan:
    def __init__(self, sizes, bands, width):
        self.sizes = sizes
        self.bands, self.width = bands, width
        self.paired = sizes[0] == 2
        self.chunks = bands // LANES
        self.rows = 3 * self.chunks
        self.plane = sizes[0] * sizes[1]
        self.share = -(-self.rows // self.plane)
        self.workers = -(-(self.rows - 1) // self.share)
        self.devices = self.plane * sizes[2]
        self.slots = 4 if self.paired else 3
        self.rounds = [size // 2 for size in sizes]


def kernel(plan, shift_hbm, a_ref, sums_ref,
           shift_ref, own, partner, rolled, diag_re, diag_im, total,
           xres, xout, rows, pooled, levels, final, every,
           shift_sem, own_sem, send_sem, recv_sem, xres_sem,
           pool_send, pool_recv, level_send, level_recv, final_send, final_recv,
           every_send, every_recv, token):
    sizes, bands, width = plan.sizes, plan.bands, plan.width
    chunks, cut = plan.chunks, LANES
    tiles, row_tiles = width // LANES, bands // ROWS
    place = [lax.axis_index(axis) for axis in AXES]
    me_plane = place[0] * sizes[1] + place[1]
    me = me_plane * sizes[2] + place[2]

    def beside(d, step):
        return {AXES[d]: lax.rem(place[d] + step, sizes[d])}

    load = pltpu.make_async_copy(a_ref, own, own_sem)
    load.start()
    shifts = pltpu.make_async_copy(shift_hbm, shift_ref, shift_sem)
    shifts.start()

    barrier = pltpu.get_barrier_semaphore()
    greetings = 0
    for d in (2, 0, 1):
        for step in sorted({1, sizes[d] - 1}):
            pl.semaphore_signal(barrier, inc=1, device_id=beside(d, step), device_id_type=MESH)
            greetings += 1
    pl.semaphore_wait(barrier, greetings)

    def copy_of(d, c):
        return pltpu.make_async_remote_copy(
            src_ref=a_ref.at[:, pl.ds(pl.multiple_of(c * cut, cut), cut), :],
            dst_ref=partner.at[d, c],
            send_sem=send_sem.at[d, c],
            recv_sem=recv_sem.at[d, c],
            device_id=beside(d, sizes[d] - 1),
            device_id_type=MESH,
        )

    if plan.paired:
        computes = lax.rem(place[0] + place[1], 2) == 0
        yields = jnp.logical_not(computes)
    else:
        computes = yields = None

    def when(condition, act):
        if condition is None:
            act()
        else:
            pl.when(condition)(act)

    for c in range(chunks):
        copy_of(2, c).start()
    for c in range(chunks):
        when(yields, lambda: copy_of(0, c).start())
        copy_of(1, c).start()

    total[...] = jnp.zeros_like(total)
    diag_re[...] = jnp.zeros_like(diag_re)
    diag_im[...] = jnp.zeros_like(diag_im)
    rows[...] = jnp.zeros_like(rows)
    shifts.wait()
    load.wait()
    for d in range(3):
        if d == 0 and plan.paired:
            shift = jnp.where(place[d] == 0, tiles - shift_ref[d], shift_ref[d])
        else:
            shift = jnp.where(place[d] == sizes[d] - 1, shift_ref[d], 0)
        moves = [(LANES << bit, (shift >> bit) & 1 == 1) for bit in range((tiles - 1).bit_length())]

        def turn(block, carry, d=d, moves=moves):
            strip = pl.ds(pl.multiple_of(block * STRIP, STRIP), STRIP)
            for part in range(2):
                value = own[part, strip, :]
                for amount, taken in moves:
                    moved = jnp.concatenate([value[:, width - amount:], value[:, :width - amount]], axis=1)
                    value = jnp.where(taken, moved, value)
                rolled[d, part, strip, :] = value
            return carry

        lax.fori_loop(0, bands // STRIP, turn, 0)

    for d in (1, 0, 2):
        steps = sorted({1, sizes[d] - 1})
        for turn_no in range(plan.rounds[d]):
            for way, step in enumerate(steps):
                pl.semaphore_signal(
                    token[d].at[turn_no, way], inc=1, device_id=beside(d, step), device_id_type=MESH
                )
            for way in range(len(steps)):
                pl.semaphore_wait(token[d].at[turn_no, way], 1)

    row = lax.broadcasted_iota(jnp.int32, (ROWS, cut), 0)
    column = lax.broadcasted_iota(jnp.int32, (ROWS, cut), 1)

    def measure(slot, left_ref, d, c, start, count):
        left = left_ref[:, pl.ds(pl.multiple_of(start, count), count), :].reshape(2 * count, width)
        right = partner[d, c].reshape(2 * cut, width)
        product = lax.dot_general(left, right, (((1,), (1,)), ((), ())), preferred_element_type=jnp.float32)
        re = product[:count, :cut] + product[count:, cut:]
        im = product[:count, cut:] - product[count:, :cut]
        squares = re * re + im * im
        total[slot] += jnp.sum(squares.reshape(count // 8, 8, cut), axis=0)
        same = row[:count] + start == column[:count] + c * cut
        diag_re[slot, pl.ds(c, 1), :] += jnp.sum(jnp.where(same, re, 0.0), axis=0, keepdims=True)
        diag_im[slot, pl.ds(c, 1), :] += jnp.sum(jnp.where(same, im, 0.0), axis=0, keepdims=True)

    def whole(slot, left_ref, d, c):
        def one(r, carry):
            measure(slot, left_ref, d, c, r * ROWS, ROWS)
            return carry
        lax.fori_loop(0, row_tiles, one, 0)

    y_slot, z_slot = plan.slots - 2, plan.slots - 1

    def chunk(c, carry):
        copy_of(1, c).wait_recv()
        whole(y_slot, rolled.at[1], 1, c)

        def along_x():
            copy_of(0, c).wait_recv()
            if plan.paired:
                whole(0, own, 0, c)
                whole(1, rolled.at[0], 0, c)
            else:
                whole(0, rolled.at[0], 0, c)

        when(computes, along_x)
        return carry

    lax.fori_loop(0, chunks, chunk, 0)

    def phases(slot, sign=None):
        im = diag_im[slot] if sign is None else sign * diag_im[slot]
        return jnp.arctan2(im, diag_re[slot])

    xres_copy = pltpu.make_async_remote_copy(
        src_ref=xout, dst_ref=xres, send_sem=xres_sem.at[0], recv_sem=xres_sem.at[1],
        device_id=beside(0, sizes[0] - 1), device_id_type=MESH,
    )
    if plan.paired:
        def share_x():
            first = place[0] == 0
            sign = jnp.where(first, 1.0, -1.0)
            low, high = phases(0, sign), phases(1, -sign)
            xres[:chunks] = jnp.where(first, low, high)
            xres[chunks:] = jnp.where(first, total[0], total[1])
            xout[:chunks] = jnp.where(first, high, low)
            xout[chunks:] = jnp.where(first, total[1], total[0])
            xres_copy.start()

        pl.when(computes)(share_x)
    else:
        xres[:chunks] = phases(0)
        xres[chunks:] = total[0]

    def along_z(c, carry):
        copy_of(2, c).wait_recv()
        whole(z_slot, rolled.at[2], 2, c)
        return carry

    last = chunks - 1
    lax.fori_loop(0, last, along_z, 0)

    if plan.paired:
        pl.when(yields)(lambda: xres_copy.wait_recv())
    found = [xres[:chunks], phases(y_slot), phases(z_slot)]
    for d in range(3):
        for c in range(chunks):
            if d * chunks + c < plan.rows - 1:
                rows[d * chunks + c] = found[d][c:c + 1]

    share, workers, plane = plan.share, plan.workers, plan.plane
    mine = pl.ds(me_plane * share, share)
    works = me_plane < workers

    def spot(p):
        return {"kx": p // sizes[1], "ky": p % sizes[1]}

    def pool_copy(source, worker):
        return pltpu.make_async_remote_copy(
            src_ref=rows.at[pl.ds(worker * share, share)], dst_ref=pooled.at[source],
            send_sem=pool_send.at[worker], recv_sem=pool_recv.at[source],
            device_id=spot(worker), device_id_type=MESH,
        )

    for worker in range(workers):
        pl.when(me_plane != worker)(lambda worker=worker: pool_copy(me_plane, worker).start())

    def level_copy(step):
        return pltpu.make_async_remote_copy(
            src_ref=levels.at[0], dst_ref=levels.at[step],
            send_sem=level_send.at[step], recv_sem=level_recv.at[step],
            device_id=beside(2, step), device_id_type=MESH,
        )

    def final_copy(worker, p):
        return pltpu.make_async_remote_copy(
            src_ref=final.at[pl.ds(worker * share, share)], dst_ref=final.at[pl.ds(worker * share, share)],
            send_sem=final_send.at[p], recv_sem=final_recv.at[worker],
            device_id=spot(p), device_id_type=MESH,
        )

    def pool():
        pooled[me_plane] = rows[mine]
        for p in range(plane):
            pl.when(me_plane != p)(lambda p=p: pool_copy(p, 0).wait_recv())
        mean = added([pooled[p] for p in range(plane)]) / plane
        square = added([(pooled[p] - mean) * (pooled[p] - mean) for p in range(plane)])
        levels[0, 0] = mean
        levels[0, 1] = square
        for step in range(1, sizes[2]):
            level_copy(step).start()

    def merge():
        for step in range(1, sizes[2]):
            level_copy(step).wait_recv()
        heard = []
        for z in range(sizes[2]):
            at = lax.rem(place[2] - z + sizes[2], sizes[2])
            heard.append((levels[at, 0], levels[at, 1]))
        mean = added([part[0] for part in heard]) / sizes[2]
        square = added([part[1] for part in heard])
        apart = added([(part[0] - mean) * (part[0] - mean) for part in heard])
        square = square + plane * apart
        for w in range(share):
            final[me_plane * share + w, 0] = mean[w]
            final[me_plane * share + w, 1] = square[w]
        for p in range(plane):
            pl.when(me_plane != p)(lambda p=p: final_copy(me_plane, p).start())

    pl.when(works)(pool)
    pl.when(works)(merge)
    for worker in range(workers):
        pl.when(me_plane != worker)(lambda worker=worker: final_copy(worker, 0).wait_recv())

    edge = bands - cut
    copy_of(2, last).wait_recv()
    measure(z_slot, rolled.at[2], 2, last, edge, cut)
    every[me] = jnp.arctan2(diag_im[z_slot, last:last + 1], diag_re[z_slot, last:last + 1])

    def every_copy(slot, x, y, z):
        return pltpu.make_async_remote_copy(
            src_ref=every.at[me], dst_ref=every.at[me],
            send_sem=every_send.at[slot], recv_sem=every_recv.at[me],
            device_id={"kx": x, "ky": y, "kz": z}, device_id_type=MESH,
        )

    def heard_from(other):
        return pltpu.make_async_remote_copy(
            src_ref=every.at[me], dst_ref=every.at[other],
            send_sem=every_send.at[0], recv_sem=every_recv.at[other],
            device_id=beside(2, 1), device_id_type=MESH,
        )

    def place_of(slot):
        return slot // (sizes[1] * sizes[2]), (slot // sizes[2]) % sizes[1], slot % sizes[2]

    def each(act):
        if plan.devices <= 64:
            for slot in range(1, plan.devices):
                act(slot)
        else:
            def one(slot, carry):
                act(slot)
                return carry
            lax.fori_loop(1, plan.devices, one, 0)

    def offset(slot):
        return [lax.rem(place[d] + step, sizes[d]) for d, step in enumerate(place_of(slot))]

    each(lambda slot: every_copy(slot, *offset(slot)).start())
    for start in range(0, edge, ROWS):
        measure(z_slot, rolled.at[2], 2, last, start, min(ROWS, edge - start))

    totals = [xres[chunks:], total[y_slot], total[z_slot]]
    for d in range(3):
        sums_ref[2 * plan.rows + 8 * d:2 * plan.rows + 8 * (d + 1), :] = totals[d]
    for r in range(plan.rows - 1):
        sums_ref[r:r + 1, :] = final[r, 0]
        sums_ref[plan.rows + r:plan.rows + r + 1, :] = final[r, 1]

    def hear(slot):
        x, y, z = offset(slot)
        heard_from((x * sizes[1] + y) * sizes[2] + z).wait_recv()

    each(hear)
    if plan.devices <= 64:
        mean = added([every[k] for k in range(plan.devices)]) / plan.devices
        square = added([(every[k] - mean) * (every[k] - mean) for k in range(plan.devices)])
    else:
        zero = jnp.zeros((1, cut), jnp.float32)
        mean = lax.fori_loop(0, plan.devices, lambda k, sofar: sofar + every[k], zero) / plan.devices
        square = lax.fori_loop(
            0, plan.devices, lambda k, sofar: sofar + (every[k] - mean) * (every[k] - mean), zero
        )
    sums_ref[plan.rows - 1:plan.rows, :] = mean
    sums_ref[2 * plan.rows - 1:2 * plan.rows, :] = square

    each(lambda slot: every_copy(slot, *offset(slot)).wait_send())
    for worker in range(workers):
        pl.when(me_plane != worker)(lambda worker=worker: pool_copy(me_plane, worker).wait_send())

    def settle():
        for step in range(1, sizes[2]):
            level_copy(step).wait_send()
        for p in range(plane):
            pl.when(me_plane != p)(lambda p=p: final_copy(me_plane, p).wait_send())

    pl.when(works)(settle)
    if plan.paired:
        pl.when(computes)(lambda: xres_copy.wait_send())

    for c in range(chunks):
        when(yields, lambda: copy_of(0, c).wait_send())
        copy_of(1, c).wait_send()
        copy_of(2, c).wait_send()


def results(plan, sums_ref, centre_ref, spread_ref, coherence_ref):
    chunks, count = plan.chunks, plan.devices
    for d in range(3):
        scale = plan.sizes[d] / (2.0 * jnp.pi)
        for c in range(chunks):
            lanes = slice(c * LANES, (c + 1) * LANES)
            at = d * chunks + c
            centre_ref[d:d + 1, lanes] = -scale * sums_ref[at:at + 1, :]
            at += plan.rows
            spread_ref[d:d + 1, lanes] = scale * scale * (sums_ref[at:at + 1, :] / count)
    for d in range(3):
        at = 2 * plan.rows + 8 * d
        coherence_ref[d] = jnp.sum(sums_ref[at:at + 8, :]) / plan.bands


def solution(mesh):
    sizes = tuple(mesh.shape[axis] for axis in AXES)

    def shards(coefficients, shift_blocks):
        bands, width = coefficients.shape[4], coefficients.shape[5]
        plan = Plan(sizes, bands, width)
        chunks = plan.chunks
        vmem = pl.BlockSpec(memory_space=pltpu.VMEM)
        hbm = pl.BlockSpec(memory_space=pl.ANY)
        dma = pltpu.SemaphoreType.DMA
        padded = plan.plane * plan.share
        sums = pl.pallas_call(
            functools.partial(kernel, plan),
            out_shape=pltpu.VMEM((2 * plan.rows + 24, LANES), jnp.float32),
            in_specs=[hbm, hbm],
            out_specs=vmem,
            scratch_shapes=[
                pltpu.SMEM((3,), jnp.int32),
                pltpu.VMEM((2, bands, width), jnp.bfloat16),
                pltpu.VMEM((3, chunks, 2, LANES, width), jnp.bfloat16),
                pltpu.VMEM((3, 2, bands, width), jnp.bfloat16),
                pltpu.VMEM((plan.slots, chunks, LANES), jnp.float32),
                pltpu.VMEM((plan.slots, chunks, LANES), jnp.float32),
                pltpu.VMEM((plan.slots, 8, LANES), jnp.float32),
                pltpu.VMEM((chunks + 8, LANES), jnp.float32),
                pltpu.VMEM((chunks + 8, LANES), jnp.float32),
                pltpu.VMEM((padded, 1, LANES), jnp.float32),
                pltpu.VMEM((plan.plane, plan.share, 1, LANES), jnp.float32),
                pltpu.VMEM((sizes[2], 2, plan.share, 1, LANES), jnp.float32),
                pltpu.VMEM((padded, 2, 1, LANES), jnp.float32),
                pltpu.VMEM((plan.devices, 1, LANES), jnp.float32),
                dma,
                dma,
                dma((3, chunks)),
                dma((3, chunks)),
                dma((2,)),
                dma((plan.workers,)),
                dma((plan.plane,)),
                dma((sizes[2],)),
                dma((sizes[2],)),
                dma((plan.plane,)),
                dma((plan.workers,)),
                dma((plan.devices,)),
                dma((plan.devices,)),
                [pltpu.SemaphoreType.REGULAR((rounds, 2)) for rounds in plan.rounds],
            ],
            compiler_params=pltpu.CompilerParams(
                collective_id=0, has_side_effects=True, vmem_limit_bytes=60 * 1024 * 1024
            ),
        )(shift_blocks, coefficients.reshape(2, bands, width))
        sums = pltpu.with_memory_space_constraint(sums, pltpu.VMEM)
        centre, spread, coherence = pl.pallas_call(
            functools.partial(results, plan),
            out_shape=(
                jax.ShapeDtypeStruct((3, bands), jnp.float32),
                jax.ShapeDtypeStruct((3, bands), jnp.float32),
                jax.ShapeDtypeStruct((3,), jnp.float32),
            ),
            in_specs=[vmem],
            out_specs=(vmem, vmem, pl.BlockSpec(memory_space=pltpu.SMEM)),
        )(sums)
        return centre, spread, coherence.reshape(3, 1, 1, 1)

    in_specs = (P(None, "kx", "ky", "kz", None, None), P())
    out_specs = (P(), P(), P(None, "kx", "ky", "kz"))
    return jax.shard_map(shards, mesh=mesh, in_specs=in_specs, out_specs=out_specs, check_vma=False)
```

time: 111 us -> 109 us (0.982)
  Pallas kernels: 110 us -> 108 us
    pallas_call x2, Pallas kernels: 110 us -> 108 us  [the longest x1 108 us: shards(): pl.pallas_call(functools.partial(kernel, plan), out_shape=pltpu.VMEM((2 *...]
where the time goes in v2:
time: 109 us
  Pallas kernels  108 us (99%)
    pallas_call x1, Pallas kernels, shards(): pl.pallas_call(functools.partial(kernel, plan), out_shape=pltpu.VMEM((2 *...  108 us

profile of v2, /device:TPU:0, one launch (start us, length us, event | category | flops | bytes accessed | tf_op | source)
XLA Modules:
  0.0 108.8 jit_solution(622285759932070364)
XLA Ops:
  0.6 107.5 %shard_map.49.sums_ref = f32[48,128]{1,0:T(8,128)S(1)} custom-call(s32[3]{0:T(128)} %shift_hbm.1, bf16[2,512,2048]{2,1,0:T(8,128)(2,1)} %bitcast.2), custom_call_target="tpu_custom_call" | custom-call | tf_op jit(solution)/shard_map/pallas_call | solution.py:381
  108.2 0.6 shard_map.50

commit v3 on v2

--- a/solution.py
+++ b/solution.py
@@ -30,12 +30,13 @@
         self.workers = -(-(self.rows - 1) // self.share)
         self.devices = self.plane * sizes[2]
         self.slots = 4 if self.paired else 3
-        self.rounds = [size // 2 for size in sizes]
+        self.toward = [sizes[0] - 1, sizes[1] - 1, 1]
+        self.half = LANES // 2
 
 
 def kernel(plan, shift_hbm, a_ref, sums_ref,
            shift_ref, own, partner, rolled, diag_re, diag_im, total,
-           xres, xout, rows, pooled, levels, final, every,
+           xres, xout, ztotal, rows, pooled, levels, final, every,
            shift_sem, own_sem, send_sem, recv_sem, xres_sem,
            pool_send, pool_recv, level_send, level_recv, final_send, final_recv,
            every_send, every_recv, token):
@@ -55,12 +56,10 @@
     shifts.start()
 
     barrier = pltpu.get_barrier_semaphore()
-    greetings = 0
     for d in (2, 0, 1):
-        for step in sorted({1, sizes[d] - 1}):
-            pl.semaphore_signal(barrier, inc=1, device_id=beside(d, step), device_id_type=MESH)
-            greetings += 1
-    pl.semaphore_wait(barrier, greetings)
+        source = beside(d, sizes[d] - plan.toward[d])
+        pl.semaphore_signal(barrier, inc=1, device_id=source, device_id_type=MESH)
+    pl.semaphore_wait(barrier, 3)
 
     def copy_of(d, c):
         return pltpu.make_async_remote_copy(
@@ -68,7 +67,19 @@
             dst_ref=partner.at[d, c],
             send_sem=send_sem.at[d, c],
             recv_sem=recv_sem.at[d, c],
-            device_id=beside(d, sizes[d] - 1),
+            device_id=beside(d, plan.toward[d]),
+            device_id_type=MESH,
+        )
+
+    last, half = chunks - 1, plan.half
+
+    def tail_copy(part):
+        return pltpu.make_async_remote_copy(
+            src_ref=a_ref.at[:, pl.ds(last * cut + part * half, half), :],
+            dst_ref=partner.at[2, last, :, pl.ds(part * half, half), :],
+            send_sem=send_sem.at[2, last + part],
+            recv_sem=recv_sem.at[2, last + part],
+            device_id=beside(2, plan.toward[2]),
             device_id_type=MESH,
         )
 
@@ -84,8 +95,9 @@
         else:
             pl.when(condition)(act)
 
-    for c in range(chunks):
+    for c in range(last):
         copy_of(2, c).start()
+    tail_copy(0).start()
     for c in range(chunks):
         when(yields, lambda: copy_of(0, c).start())
         copy_of(1, c).start()
@@ -99,6 +111,8 @@
     for d in range(3):
         if d == 0 and plan.paired:
             shift = jnp.where(place[d] == 0, tiles - shift_ref[d], shift_ref[d])
+        elif d == 2:
+            shift = jnp.where(place[d] == 0, tiles - shift_ref[d], 0)
         else:
             shift = jnp.where(place[d] == sizes[d] - 1, shift_ref[d], 0)
         moves = [(LANES << bit, (shift >> bit) & 1 == 1) for bit in range((tiles - 1).bit_length())]
@@ -116,14 +130,11 @@
         lax.fori_loop(0, bands // STRIP, turn, 0)
 
     for d in (1, 0, 2):
-        steps = sorted({1, sizes[d] - 1})
-        for turn_no in range(plan.rounds[d]):
-            for way, step in enumerate(steps):
-                pl.semaphore_signal(
-                    token[d].at[turn_no, way], inc=1, device_id=beside(d, step), device_id_type=MESH
-                )
-            for way in range(len(steps)):
-                pl.semaphore_wait(token[d].at[turn_no, way], 1)
+        for turn_no in range(sizes[d] - 1):
+            pl.semaphore_signal(
+                token[d].at[turn_no], inc=1, device_id=beside(d, plan.toward[d]), device_id_type=MESH
+            )
+            pl.semaphore_wait(token[d].at[turn_no], 1)
 
     row = lax.broadcasted_iota(jnp.int32, (ROWS, cut), 0)
     column = lax.broadcasted_iota(jnp.int32, (ROWS, cut), 1)
@@ -194,12 +205,11 @@
         whole(z_slot, rolled.at[2], 2, c)
         return carry
 
-    last = chunks - 1
     lax.fori_loop(0, last, along_z, 0)
 
     if plan.paired:
         pl.when(yields)(lambda: xres_copy.wait_recv())
-    found = [xres[:chunks], phases(y_slot), phases(z_slot)]
+    found = [xres[:chunks], phases(y_slot), phases(z_slot, -1.0)]
     for d in range(3):
         for c in range(chunks):
             if d * chunks + c < plan.rows - 1:
@@ -265,14 +275,16 @@
             pl.when(me_plane != p)(lambda p=p: final_copy(me_plane, p).start())
 
     pl.when(works)(pool)
+    tail_copy(1).start()
     pl.when(works)(merge)
     for worker in range(workers):
         pl.when(me_plane != worker)(lambda worker=worker: final_copy(worker, 0).wait_recv())
 
     edge = bands - cut
-    copy_of(2, last).wait_recv()
+    for part in range(2):
+        tail_copy(part).wait_recv()
     measure(z_slot, rolled.at[2], 2, last, edge, cut)
-    every[me] = jnp.arctan2(diag_im[z_slot, last:last + 1], diag_re[z_slot, last:last + 1])
+    every[me] = jnp.arctan2(-diag_im[z_slot, last:last + 1], diag_re[z_slot, last:last + 1])
 
     def every_copy(slot, x, y, z):
         return pltpu.make_async_remote_copy(
@@ -308,12 +320,14 @@
     for start in range(0, edge, ROWS):
         measure(z_slot, rolled.at[2], 2, last, start, min(ROWS, edge - start))
 
-    totals = [xres[chunks:], total[y_slot], total[z_slot]]
-    for d in range(3):
-        sums_ref[2 * plan.rows + 8 * d:2 * plan.rows + 8 * (d + 1), :] = totals[d]
+    ztotal_copy = pltpu.make_async_remote_copy(
+        src_ref=total.at[z_slot], dst_ref=ztotal, send_sem=xres_sem.at[2], recv_sem=xres_sem.at[3],
+        device_id=beside(2, sizes[2] - plan.toward[2]), device_id_type=MESH,
+    )
     for r in range(plan.rows - 1):
         sums_ref[r:r + 1, :] = final[r, 0]
         sums_ref[plan.rows + r:plan.rows + r + 1, :] = final[r, 1]
+    ztotal_copy.start()
 
     def hear(slot):
         x, y, z = offset(slot)
@@ -329,6 +343,10 @@
         square = lax.fori_loop(
             0, plan.devices, lambda k, sofar: sofar + (every[k] - mean) * (every[k] - mean), zero
         )
+    ztotal_copy.wait_recv()
+    totals = [xres[chunks:], total[y_slot], ztotal[...]]
+    for d in range(3):
+        sums_ref[2 * plan.rows + 8 * d:2 * plan.rows + 8 * (d + 1), :] = totals[d]
     sums_ref[plan.rows - 1:plan.rows, :] = mean
     sums_ref[2 * plan.rows - 1:2 * plan.rows, :] = square
 
@@ -349,7 +367,11 @@
     for c in range(chunks):
         when(yields, lambda: copy_of(0, c).wait_send())
         copy_of(1, c).wait_send()
-        copy_of(2, c).wait_send()
+        if c < last:
+            copy_of(2, c).wait_send()
+    for part in range(2):
+        tail_copy(part).wait_send()
+    ztotal_copy.wait_send()
 
 
 def results(plan, sums_ref, centre_ref, spread_ref, coherence_ref):
@@ -393,6 +415,7 @@
                 pltpu.VMEM((plan.slots, 8, LANES), jnp.float32),
                 pltpu.VMEM((chunks + 8, LANES), jnp.float32),
                 pltpu.VMEM((chunks + 8, LANES), jnp.float32),
+                pltpu.VMEM((8, LANES), jnp.float32),
                 pltpu.VMEM((padded, 1, LANES), jnp.float32),
                 pltpu.VMEM((plan.plane, plan.share, 1, LANES), jnp.float32),
                 pltpu.VMEM((sizes[2], 2, plan.share, 1, LANES), jnp.float32),
@@ -400,9 +423,9 @@
                 pltpu.VMEM((plan.devices, 1, LANES), jnp.float32),
                 dma,
                 dma,
-                dma((3, chunks)),
-                dma((3, chunks)),
-                dma((2,)),
+                dma((3, chunks + 1)),
+                dma((3, chunks + 1)),
+                dma((4,)),
                 dma((plan.workers,)),
                 dma((plan.plane,)),
                 dma((sizes[2],)),
@@ -411,7 +434,7 @@
                 dma((plan.workers,)),
                 dma((plan.devices,)),
                 dma((plan.devices,)),
-                [pltpu.SemaphoreType.REGULAR((rounds, 2)) for rounds in plan.rounds],
+                [pltpu.SemaphoreType.REGULAR((size - 1,)) for size in sizes],
             ],
             compiler_params=pltpu.CompilerParams(
                 collective_id=0, has_side_effects=True, vmem_limit_bytes=60 * 1024 * 1024

time: 109 us -> 105 us (0.963)
  Pallas kernels: 108 us -> 104 us
    pallas_call x1, Pallas kernels: 108 us -> 103 us  [shards(): pl.pallas_call(functools.partial(kernel, plan), out_shape=pltpu.VMEM((2 *...]
where the time goes in v3:
time: 105 us
  Pallas kernels  104 us (99%)
    pallas_call x1, Pallas kernels, shards(): pl.pallas_call(functools.partial(kernel, plan), out_shape=pltpu.VMEM((2 *...  103 us

profile of v3, /device:TPU:0, one launch (start us, length us, event | category | flops | bytes accessed | tf_op | source)
XLA Modules:
  0.0 104.7 jit_solution(9602606629438349994)
XLA Ops:
  0.6 103.4 %shard_map.49.sums_ref = f32[48,128]{1,0:T(8,128)S(1)} custom-call(s32[3]{0:T(128)} %shift_hbm.1, bf16[2,512,2048]{2,1,0:T(8,128)(2,1)} %bitcast.2), custom_call_target="tpu_custom_call" | custom-call | tf_op jit(solution)/shard_map/pallas_call | solution.py:403
  104.1 0.6 shard_map.50

commit v4 on v3

--- a/solution.py
+++ b/solution.py
@@ -15,7 +15,9 @@
 
 
 def added(parts):
-    return functools.reduce(jnp.add, parts)
+    while len(parts) > 1:
+        parts = [a + b for a, b in zip(parts[::2], parts[1::2])] + parts[len(parts) // 2 * 2:]
+    return parts[0]
 
 
 class Plan:
@@ -31,15 +33,14 @@
         self.devices = self.plane * sizes[2]
         self.slots = 4 if self.paired else 3
         self.toward = [sizes[0] - 1, sizes[1] - 1, 1]
-        self.half = LANES // 2
+        self.parts = ((0, 64), (64, 32), (96, 32))
 
 
 def kernel(plan, shift_hbm, a_ref, sums_ref,
            shift_ref, own, partner, rolled, diag_re, diag_im, total,
            xres, xout, ztotal, rows, pooled, levels, final, every,
            shift_sem, own_sem, send_sem, recv_sem, xres_sem,
-           pool_send, pool_recv, level_send, level_recv, final_send, final_recv,
-           every_send, every_recv, token):
+           share_sem, every_sem, token):
     sizes, bands, width = plan.sizes, plan.bands, plan.width
     chunks, cut = plan.chunks, LANES
     tiles, row_tiles = width // LANES, bands // ROWS
@@ -65,23 +66,27 @@
         return pltpu.make_async_remote_copy(
             src_ref=a_ref.at[:, pl.ds(pl.multiple_of(c * cut, cut), cut), :],
             dst_ref=partner.at[d, c],
-            send_sem=send_sem.at[d, c],
+            send_sem=send_sem.at[d],
             recv_sem=recv_sem.at[d, c],
             device_id=beside(d, plan.toward[d]),
             device_id_type=MESH,
         )
 
-    last, half = chunks - 1, plan.half
+    last, parts = chunks - 1, plan.parts
 
     def tail_copy(part):
-        return pltpu.make_async_remote_copy(
-            src_ref=a_ref.at[:, pl.ds(last * cut + part * half, half), :],
-            dst_ref=partner.at[2, last, :, pl.ds(part * half, half), :],
-            send_sem=send_sem.at[2, last + part],
+        low, span = parts[part]
+        return pltpu.make_async_remote_copy(
+            src_ref=a_ref.at[:, pl.ds(last * cut + low, span), :],
+            dst_ref=partner.at[2, last, :, pl.ds(low, span), :],
+            send_sem=send_sem.at[2],
             recv_sem=recv_sem.at[2, last + part],
             device_id=beside(2, plan.toward[2]),
             device_id_type=MESH,
         )
+
+    def bulk(ref, semaphore):
+        return pltpu.make_async_copy(ref, ref, semaphore)
 
     if plan.paired:
         computes = lax.rem(place[0] + place[1], 2) == 0
@@ -132,28 +137,30 @@
     for d in (1, 0, 2):
         for turn_no in range(sizes[d] - 1):
             pl.semaphore_signal(
-                token[d].at[turn_no], inc=1, device_id=beside(d, plan.toward[d]), device_id_type=MESH
+                token.at[d], inc=1, device_id=beside(d, plan.toward[d]), device_id_type=MESH
             )
-            pl.semaphore_wait(token[d].at[turn_no], 1)
+            pl.semaphore_wait(token.at[d], 1)
 
     row = lax.broadcasted_iota(jnp.int32, (ROWS, cut), 0)
     column = lax.broadcasted_iota(jnp.int32, (ROWS, cut), 1)
 
-    def measure(slot, left_ref, d, c, start, count):
-        left = left_ref[:, pl.ds(pl.multiple_of(start, count), count), :].reshape(2 * count, width)
-        right = partner[d, c].reshape(2 * cut, width)
+    def measure(slot, left_ref, d, c, start, count, lanes=(0, LANES)):
+        low, span = lanes
+        first = start if isinstance(start, int) else pl.multiple_of(start, count)
+        left = left_ref[:, pl.ds(first, count), :].reshape(2 * count, width)
+        right = partner[d, c, :, low:low + span].reshape(2 * span, width)
         product = lax.dot_general(left, right, (((1,), (1,)), ((), ())), preferred_element_type=jnp.float32)
-        re = product[:count, :cut] + product[count:, cut:]
-        im = product[:count, cut:] - product[count:, :cut]
+        re = product[:count, :span] + product[count:, span:]
+        im = product[:count, span:] - product[count:, :span]
         squares = re * re + im * im
-        total[slot] += jnp.sum(squares.reshape(count // 8, 8, cut), axis=0)
-        same = row[:count] + start == column[:count] + c * cut
-        diag_re[slot, pl.ds(c, 1), :] += jnp.sum(jnp.where(same, re, 0.0), axis=0, keepdims=True)
-        diag_im[slot, pl.ds(c, 1), :] += jnp.sum(jnp.where(same, im, 0.0), axis=0, keepdims=True)
-
-    def whole(slot, left_ref, d, c):
+        total[slot, :, :span] += jnp.sum(squares.reshape(count // 8, 8, span), axis=0)
+        same = row[:count, :span] + start == column[:count, :span] + (c * cut + low)
+        diag_re[slot, pl.ds(c, 1), low:low + span] += jnp.sum(jnp.where(same, re, 0.0), axis=0, keepdims=True)
+        diag_im[slot, pl.ds(c, 1), low:low + span] += jnp.sum(jnp.where(same, im, 0.0), axis=0, keepdims=True)
+
+    def whole(slot, left_ref, d, c, lanes=(0, LANES)):
         def one(r, carry):
-            measure(slot, left_ref, d, c, r * ROWS, ROWS)
+            measure(slot, left_ref, d, c, r * ROWS, ROWS, lanes)
             return carry
         lax.fori_loop(0, row_tiles, one, 0)
 
@@ -217,7 +224,7 @@
 
     share, workers, plane = plan.share, plan.workers, plan.plane
     mine = pl.ds(me_plane * share, share)
-    works = me_plane < workers
+    works, idles = me_plane < workers, me_plane >= workers
 
     def spot(p):
         return {"kx": p // sizes[1], "ky": p % sizes[1]}
@@ -225,7 +232,7 @@
     def pool_copy(source, worker):
         return pltpu.make_async_remote_copy(
             src_ref=rows.at[pl.ds(worker * share, share)], dst_ref=pooled.at[source],
-            send_sem=pool_send.at[worker], recv_sem=pool_recv.at[source],
+            send_sem=share_sem.at[0], recv_sem=share_sem.at[1],
             device_id=spot(worker), device_id_type=MESH,
         )
 
@@ -235,21 +242,20 @@
     def level_copy(step):
         return pltpu.make_async_remote_copy(
             src_ref=levels.at[0], dst_ref=levels.at[step],
-            send_sem=level_send.at[step], recv_sem=level_recv.at[step],
+            send_sem=share_sem.at[2], recv_sem=share_sem.at[3],
             device_id=beside(2, step), device_id_type=MESH,
         )
 
     def final_copy(worker, p):
         return pltpu.make_async_remote_copy(
             src_ref=final.at[pl.ds(worker * share, share)], dst_ref=final.at[pl.ds(worker * share, share)],
-            send_sem=final_send.at[p], recv_sem=final_recv.at[worker],
+            send_sem=share_sem.at[4], recv_sem=share_sem.at[5],
             device_id=spot(p), device_id_type=MESH,
         )
 
     def pool():
         pooled[me_plane] = rows[mine]
-        for p in range(plane):
-            pl.when(me_plane != p)(lambda p=p: pool_copy(p, 0).wait_recv())
+        bulk(pooled.at[pl.ds(0, plane - 1)], share_sem.at[1]).wait()
         mean = added([pooled[p] for p in range(plane)]) / plane
         square = added([(pooled[p] - mean) * (pooled[p] - mean) for p in range(plane)])
         levels[0, 0] = mean
@@ -258,8 +264,7 @@
             level_copy(step).start()
 
     def merge():
-        for step in range(1, sizes[2]):
-            level_copy(step).wait_recv()
+        bulk(levels.at[pl.ds(0, sizes[2] - 1)], share_sem.at[3]).wait()
         heard = []
         for z in range(sizes[2]):
             at = lax.rem(place[2] - z + sizes[2], sizes[2])
@@ -275,103 +280,95 @@
             pl.when(me_plane != p)(lambda p=p: final_copy(me_plane, p).start())
 
     pl.when(works)(pool)
-    tail_copy(1).start()
+    for part in range(1, len(parts)):
+        tail_copy(part).start()
     pl.when(works)(merge)
-    for worker in range(workers):
-        pl.when(me_plane != worker)(lambda worker=worker: final_copy(worker, 0).wait_recv())
-
-    edge = bands - cut
-    for part in range(2):
+    pl.when(works)(lambda: bulk(final.at[pl.ds(0, (workers - 1) * share)], share_sem.at[5]).wait())
+    pl.when(idles)(lambda: bulk(final.at[pl.ds(0, workers * share)], share_sem.at[5]).wait())
+
+    for r in range(plan.rows - 1):
+        sums_ref[r:r + 1, :] = final[r, 0]
+        sums_ref[plan.rows + r:plan.rows + r + 1, :] = final[r, 1]
+    pl.when(works)(lambda: bulk(rows.at[pl.ds(0, (workers - 1) * share)], share_sem.at[0]).wait())
+    pl.when(idles)(lambda: bulk(rows.at[pl.ds(0, workers * share)], share_sem.at[0]).wait())
+
+    def settle():
+        bulk(levels.at[pl.ds(0, sizes[2] - 1)], share_sem.at[2]).wait()
+        bulk(final.at[pl.ds(0, (plane - 1) * share)], share_sem.at[4]).wait()
+
+    pl.when(works)(settle)
+    if plan.paired:
+        pl.when(computes)(lambda: xres_copy.wait_send())
+    when(yields, lambda: bulk(own, send_sem.at[0]).wait())
+    bulk(own, send_sem.at[1]).wait()
+    for part in range(len(parts) - 1):
         tail_copy(part).wait_recv()
-    measure(z_slot, rolled.at[2], 2, last, edge, cut)
+        whole(z_slot, rolled.at[2], 2, last, parts[part])
+
+    lanes = parts[-1]
+    edge = bands - lanes[1]
+    tail_copy(len(parts) - 1).wait_recv()
+    measure(z_slot, rolled.at[2], 2, last, edge, lanes[1], lanes)
     every[me] = jnp.arctan2(-diag_im[z_slot, last:last + 1], diag_re[z_slot, last:last + 1])
 
-    def every_copy(slot, x, y, z):
+    def place_of(k):
+        return (k // sizes[1]) % sizes[0], k % sizes[1], k // plane
+
+    def slot_of(k):
+        x, y, z = place_of(k)
+        return (x * sizes[1] + y) * sizes[2] + z
+
+    def every_copy(k):
+        x, y, z = place_of(k)
         return pltpu.make_async_remote_copy(
             src_ref=every.at[me], dst_ref=every.at[me],
-            send_sem=every_send.at[slot], recv_sem=every_recv.at[me],
+            send_sem=every_sem.at[0], recv_sem=every_sem.at[1],
             device_id={"kx": x, "ky": y, "kz": z}, device_id_type=MESH,
         )
 
-    def heard_from(other):
-        return pltpu.make_async_remote_copy(
-            src_ref=every.at[me], dst_ref=every.at[other],
-            send_sem=every_send.at[0], recv_sem=every_recv.at[other],
-            device_id=beside(2, 1), device_id_type=MESH,
-        )
-
-    def place_of(slot):
-        return slot // (sizes[1] * sizes[2]), (slot // sizes[2]) % sizes[1], slot % sizes[2]
+    few = plan.devices <= 64
 
     def each(act):
-        if plan.devices <= 64:
-            for slot in range(1, plan.devices):
-                act(slot)
+        def one(k, carry=0):
+            pl.when(me != slot_of(k))(lambda: act(k))
+            return carry
+        if few:
+            for k in range(plan.devices):
+                one(k)
         else:
-            def one(slot, carry):
-                act(slot)
-                return carry
-            lax.fori_loop(1, plan.devices, one, 0)
-
-    def offset(slot):
-        return [lax.rem(place[d] + step, sizes[d]) for d, step in enumerate(place_of(slot))]
-
-    each(lambda slot: every_copy(slot, *offset(slot)).start())
+            lax.fori_loop(0, plan.devices, one, 0)
+
+    each(lambda k: every_copy(k).start())
     for start in range(0, edge, ROWS):
-        measure(z_slot, rolled.at[2], 2, last, start, min(ROWS, edge - start))
-
+        measure(z_slot, rolled.at[2], 2, last, start, min(ROWS, edge - start), lanes)
     ztotal_copy = pltpu.make_async_remote_copy(
         src_ref=total.at[z_slot], dst_ref=ztotal, send_sem=xres_sem.at[2], recv_sem=xres_sem.at[3],
         device_id=beside(2, sizes[2] - plan.toward[2]), device_id_type=MESH,
     )
-    for r in range(plan.rows - 1):
-        sums_ref[r:r + 1, :] = final[r, 0]
-        sums_ref[plan.rows + r:plan.rows + r + 1, :] = final[r, 1]
     ztotal_copy.start()
-
-    def hear(slot):
-        x, y, z = offset(slot)
-        heard_from((x * sizes[1] + y) * sizes[2] + z).wait_recv()
-
-    each(hear)
-    if plan.devices <= 64:
-        mean = added([every[k] for k in range(plan.devices)]) / plan.devices
-        square = added([(every[k] - mean) * (every[k] - mean) for k in range(plan.devices)])
+    at = 2 * plan.rows
+    sums_ref[at:at + 8, :] = xres[chunks:]
+    sums_ref[at + 8:at + 16, :] = total[y_slot]
+    bulk(own, send_sem.at[2]).wait()
+    others = every.at[pl.ds(0, plan.devices - 1)]
+    bulk(others, every_sem.at[0]).wait()
+    ztotal_copy.wait_send()
+    ztotal_copy.wait_recv()
+    sums_ref[at + 16:at + 24, :] = ztotal[...]
+
+    bulk(others, every_sem.at[1]).wait()
+    if few:
+        heard = [every[k] for k in range(plan.devices)]
+        mean = added(heard) / plan.devices
+        square = added([(phase - mean) * (phase - mean) for phase in heard])
     else:
         zero = jnp.zeros((1, cut), jnp.float32)
         mean = lax.fori_loop(0, plan.devices, lambda k, sofar: sofar + every[k], zero) / plan.devices
         square = lax.fori_loop(
             0, plan.devices, lambda k, sofar: sofar + (every[k] - mean) * (every[k] - mean), zero
         )
-    ztotal_copy.wait_recv()
-    totals = [xres[chunks:], total[y_slot], ztotal[...]]
-    for d in range(3):
-        sums_ref[2 * plan.rows + 8 * d:2 * plan.rows + 8 * (d + 1), :] = totals[d]
     sums_ref[plan.rows - 1:plan.rows, :] = mean
     sums_ref[2 * plan.rows - 1:2 * plan.rows, :] = square
-
-    each(lambda slot: every_copy(slot, *offset(slot)).wait_send())
-    for worker in range(workers):
-        pl.when(me_plane != worker)(lambda worker=worker: pool_copy(me_plane, worker).wait_send())
-
-    def settle():
-        for step in range(1, sizes[2]):
-            level_copy(step).wait_send()
-        for p in range(plane):
-            pl.when(me_plane != p)(lambda p=p: final_copy(me_plane, p).wait_send())
-
-    pl.when(works)(settle)
-    if plan.paired:
-        pl.when(computes)(lambda: xres_copy.wait_send())
-
-    for c in range(chunks):
-        when(yields, lambda: copy_of(0, c).wait_send())
-        copy_of(1, c).wait_send()
-        if c < last:
-            copy_of(2, c).wait_send()
-    for part in range(2):
-        tail_copy(part).wait_send()
-    ztotal_copy.wait_send()
 
 
 def results(plan, sums_ref, centre_ref, spread_ref, coherence_ref):
@@ -423,18 +420,12 @@
                 pltpu.VMEM((plan.devices, 1, LANES), jnp.float32),
                 dma,
                 dma,
-                dma((3, chunks + 1)),
-                dma((3, chunks + 1)),
+                dma((3,)),
+                dma((3, chunks + len(plan.parts) - 1)),
                 dma((4,)),
-                dma((plan.workers,)),
-                dma((plan.plane,)),
-                dma((sizes[2],)),
-                dma((sizes[2],)),
-                dma((plan.plane,)),
-                dma((plan.workers,)),
-                dma((plan.devices,)),
-                dma((plan.devices,)),
-                [pltpu.SemaphoreType.REGULAR((size - 1,)) for size in sizes],
+                dma((6,)),
+                dma((2,)),
+                pltpu.SemaphoreType.REGULAR((3,)),
             ],
             compiler_params=pltpu.CompilerParams(
                 collective_id=0, has_side_effects=True, vmem_limit_bytes=60 * 1024 * 1024

time: 105 us -> 103 us (0.981)
    pallas_call x1, Pallas kernels: 103 us -> 102 us  [shards(): pl.pallas_call(functools.partial(kernel, plan), out_shape=pltpu.VMEM((2 *...]
where the time goes in v4:
time: 103 us
  Pallas kernels  103 us (100%)
    pallas_call x1, Pallas kernels, shards(): pl.pallas_call(functools.partial(kernel, plan), out_shape=pltpu.VMEM((2 *...  102 us

profile of v4, /device:TPU:0, one launch (start us, length us, event | category | flops | bytes accessed | tf_op | source)
XLA Modules:
  0.0 103.2 jit_solution(11928592938261014403)
XLA Ops:
  0.6 102.0 %shard_map.49.sums_ref = f32[48,128]{1,0:T(8,128)S(1)} custom-call(s32[3]{0:T(128)} %shift_hbm.1, bf16[2,512,2048]{2,1,0:T(8,128)(2,1)} %bitcast.2), custom_call_target="tpu_custom_call" | custom-call | tf_op jit(solution)/shard_map/pallas_call | solution.py:400
  102.6 0.6 shard_map.50

commit v5 on v4

--- a/solution.py
+++ b/solution.py
@@ -36,7 +36,7 @@
         self.parts = ((0, 64), (64, 32), (96, 32))
 
 
-def kernel(plan, shift_hbm, a_ref, sums_ref,
+def kernel(plan, shift_hbm, a_ref, centre_ref, spread_ref, coherence_ref,
            shift_ref, own, partner, rolled, diag_re, diag_im, total,
            xres, xout, ztotal, rows, pooled, levels, final, every,
            shift_sem, own_sem, send_sem, recv_sem, xres_sem,
@@ -51,20 +51,27 @@
     def beside(d, step):
         return {AXES[d]: lax.rem(place[d] + step, sizes[d])}
 
-    load = pltpu.make_async_copy(a_ref, own, own_sem)
-    load.start()
-    shifts = pltpu.make_async_copy(shift_hbm, shift_ref, shift_sem)
-    shifts.start()
+    def load(k):
+        low, span = ((0, cut), (cut, bands - cut))[k]
+        piece = pl.ds(low, span)
+        return pltpu.make_async_copy(a_ref.at[:, piece, :], own.at[:, piece, :], own_sem.at[k])
 
     barrier = pltpu.get_barrier_semaphore()
     for d in (2, 0, 1):
         source = beside(d, sizes[d] - plan.toward[d])
         pl.semaphore_signal(barrier, inc=1, device_id=source, device_id_type=MESH)
+    for k in range(2):
+        load(k).start()
+    shifts = pltpu.make_async_copy(shift_hbm, shift_ref, shift_sem)
+    shifts.start()
     pl.semaphore_wait(barrier, 3)
 
+    def rows_of(c):
+        return pl.ds(pl.multiple_of(c * cut, cut), cut)
+
     def copy_of(d, c):
         return pltpu.make_async_remote_copy(
-            src_ref=a_ref.at[:, pl.ds(pl.multiple_of(c * cut, cut), cut), :],
+            src_ref=(own if d == 2 and isinstance(c, int) and c == 0 else a_ref).at[:, rows_of(c), :],
             dst_ref=partner.at[d, c],
             send_sem=send_sem.at[d],
             recv_sem=recv_sem.at[d, c],
@@ -100,6 +107,7 @@
         else:
             pl.when(condition)(act)
 
+    load(0).wait()
     for c in range(last):
         copy_of(2, c).start()
     tail_copy(0).start()
@@ -112,7 +120,7 @@
     diag_im[...] = jnp.zeros_like(diag_im)
     rows[...] = jnp.zeros_like(rows)
     shifts.wait()
-    load.wait()
+    load(1).wait()
     for d in range(3):
         if d == 0 and plan.paired:
             shift = jnp.where(place[d] == 0, tiles - shift_ref[d], shift_ref[d])
@@ -286,9 +294,19 @@
     pl.when(works)(lambda: bulk(final.at[pl.ds(0, (workers - 1) * share)], share_sem.at[5]).wait())
     pl.when(idles)(lambda: bulk(final.at[pl.ds(0, workers * share)], share_sem.at[5]).wait())
 
+    def settled(r, mean, square):
+        d, lanes = r // chunks, slice(r % chunks * cut, (r % chunks + 1) * cut)
+        scale = sizes[d] / (2.0 * jnp.pi)
+        centre_ref[d:d + 1, lanes] = -scale * mean
+        spread_ref[d:d + 1, lanes] = scale * scale * (square / plan.devices)
+
+    def norm(squares):
+        return jnp.sum(jnp.sum(squares, axis=0, keepdims=True), axis=1, keepdims=True) / bands
+
     for r in range(plan.rows - 1):
-        sums_ref[r:r + 1, :] = final[r, 0]
-        sums_ref[plan.rows + r:plan.rows + r + 1, :] = final[r, 1]
+        settled(r, final[r, 0], final[r, 1])
+    coherence_ref[:, 0:1] = norm(xres[chunks:])
+    coherence_ref[:, 1:2] = norm(total[y_slot])
     pl.when(works)(lambda: bulk(rows.at[pl.ds(0, (workers - 1) * share)], share_sem.at[0]).wait())
     pl.when(idles)(lambda: bulk(rows.at[pl.ds(0, workers * share)], share_sem.at[0]).wait())
 
@@ -346,15 +364,12 @@
         device_id=beside(2, sizes[2] - plan.toward[2]), device_id_type=MESH,
     )
     ztotal_copy.start()
-    at = 2 * plan.rows
-    sums_ref[at:at + 8, :] = xres[chunks:]
-    sums_ref[at + 8:at + 16, :] = total[y_slot]
     bulk(own, send_sem.at[2]).wait()
     others = every.at[pl.ds(0, plan.devices - 1)]
     bulk(others, every_sem.at[0]).wait()
     ztotal_copy.wait_send()
     ztotal_copy.wait_recv()
-    sums_ref[at + 16:at + 24, :] = ztotal[...]
+    coherence_ref[:, 2:3] = norm(ztotal[...])
 
     bulk(others, every_sem.at[1]).wait()
     if few:
@@ -367,23 +382,16 @@
         square = lax.fori_loop(
             0, plan.devices, lambda k, sofar: sofar + (every[k] - mean) * (every[k] - mean), zero
         )
-    sums_ref[plan.rows - 1:plan.rows, :] = mean
-    sums_ref[2 * plan.rows - 1:2 * plan.rows, :] = square
-
-
-def results(plan, sums_ref, centre_ref, spread_ref, coherence_ref):
-    chunks, count = plan.chunks, plan.devices
-    for d in range(3):
-        scale = plan.sizes[d] / (2.0 * jnp.pi)
-        for c in range(chunks):
-            lanes = slice(c * LANES, (c + 1) * LANES)
-            at = d * chunks + c
-            centre_ref[d:d + 1, lanes] = -scale * sums_ref[at:at + 1, :]
-            at += plan.rows
-            spread_ref[d:d + 1, lanes] = scale * scale * (sums_ref[at:at + 1, :] / count)
-    for d in range(3):
-        at = 2 * plan.rows + 8 * d
-        coherence_ref[d] = jnp.sum(sums_ref[at:at + 8, :]) / plan.bands
+    settled(plan.rows - 1, mean, square)
+
+
+def results(held_centre, held_spread, held_coherence, centre_ref, spread_ref, coherence_ref, sems):
+    pairs = ((held_centre, centre_ref), (held_spread, spread_ref), (held_coherence, coherence_ref))
+    copies = [pltpu.make_async_copy(held, out, sems.at[k]) for k, (held, out) in enumerate(pairs)]
+    for copy in copies:
+        copy.start()
+    for copy in copies:
+        copy.wait()
 
 
 def solution(mesh):
@@ -397,11 +405,12 @@
         hbm = pl.BlockSpec(memory_space=pl.ANY)
         dma = pltpu.SemaphoreType.DMA
         padded = plan.plane * plan.share
-        sums = pl.pallas_call(
+        shapes = ((3, bands), (3, bands), (1, 3))
+        held = pl.pallas_call(
             functools.partial(kernel, plan),
-            out_shape=pltpu.VMEM((2 * plan.rows + 24, LANES), jnp.float32),
+            out_shape=tuple(pltpu.VMEM(shape, jnp.float32) for shape in shapes),
             in_specs=[hbm, hbm],
-            out_specs=vmem,
+            out_specs=(vmem, vmem, vmem),
             scratch_shapes=[
                 pltpu.SMEM((3,), jnp.int32),
                 pltpu.VMEM((2, bands, width), jnp.bfloat16),
@@ -419,7 +428,7 @@
                 pltpu.VMEM((padded, 2, 1, LANES), jnp.float32),
                 pltpu.VMEM((plan.devices, 1, LANES), jnp.float32),
                 dma,
-                dma,
+                dma((2,)),
                 dma((3,)),
                 dma((3, chunks + len(plan.parts) - 1)),
                 dma((4,)),
@@ -431,17 +440,14 @@
                 collective_id=0, has_side_effects=True, vmem_limit_bytes=60 * 1024 * 1024
             ),
         )(shift_blocks, coefficients.reshape(2, bands, width))
-        sums = pltpu.with_memory_space_constraint(sums, pltpu.VMEM)
+        held = [pltpu.with_memory_space_constraint(array, pltpu.VMEM) for array in held]
         centre, spread, coherence = pl.pallas_call(
-            functools.partial(results, plan),
-            out_shape=(
-                jax.ShapeDtypeStruct((3, bands), jnp.float32),
-                jax.ShapeDtypeStruct((3, bands), jnp.float32),
-                jax.ShapeDtypeStruct((3,), jnp.float32),
-            ),
-            in_specs=[vmem],
-            out_specs=(vmem, vmem, pl.BlockSpec(memory_space=pltpu.SMEM)),
-        )(sums)
+            results,
+            out_shape=tuple(jax.ShapeDtypeStruct(shape, jnp.float32) for shape in shapes),
+            in_specs=[vmem, vmem, vmem],
+            out_specs=(hbm, hbm, hbm),
+            scratch_shapes=[dma((3,))],
+        )(*held)
         return centre, spread, coherence.reshape(3, 1, 1, 1)
 
     in_specs = (P(None, "kx", "ky", "kz", None, None), P())

time: 103 us -> 103 us (level)
  no operation moved by 1% of the time
where the time goes in v5:
time: 103 us
  Pallas kernels  103 us (100%)
    pallas_call x1, Pallas kernels, shards(): pl.pallas_call(functools.partial(kernel, plan), out_shape=tuple((pltpu.VM...  102 us

profile of v5, /device:TPU:0, one launch (start us, length us, event | category | flops | bytes accessed | tf_op | source)
XLA Modules:
  0.0 103.2 jit_solution(5113469860711970567)
XLA Ops:
  0.6 101.9 %shard_map.49 = (f32[3,512]{1,0:T(4,128)S(1)}, f32[3,512]{1,0:T(4,128)S(1)}, f32[1,3]{1,0:T(1,128)S(1)}) custom-call(s32[3]{0:T(128)} %shift_hbm.1, bf16[2,512,2048]{2,1,0:T(8,128)(2,1)} %bitcast.2), custom_call_target="tpu_custom_call" | custom-call | tf_op jit(solution)/shard_map/pallas_call | solution.py:409
  102.5 0.6 shard_map.50

commit v6 on v5

--- a/solution.py
+++ b/solution.py
@@ -57,21 +57,33 @@
         return pltpu.make_async_copy(a_ref.at[:, piece, :], own.at[:, piece, :], own_sem.at[k])
 
     barrier = pltpu.get_barrier_semaphore()
-    for d in (2, 0, 1):
-        source = beside(d, sizes[d] - plan.toward[d])
-        pl.semaphore_signal(barrier, inc=1, device_id=source, device_id_type=MESH)
+    top = place[2] == sizes[2] - 1
+    below = place[2] == sizes[2] - 2
+    lower = place[2] < sizes[2] - 1
+
+    def source(d):
+        return beside(d, sizes[d] - plan.toward[d])
+
+    pl.semaphore_signal(barrier, inc=1, device_id=source(2), device_id_type=MESH)
+
+    def greet():
+        for d in range(2):
+            pl.semaphore_signal(barrier, inc=1, device_id=source(d), device_id_type=MESH)
+
+    pl.when(lower)(greet)
     for k in range(2):
         load(k).start()
     shifts = pltpu.make_async_copy(shift_hbm, shift_ref, shift_sem)
     shifts.start()
-    pl.semaphore_wait(barrier, 3)
+    pl.when(lower)(lambda: pl.semaphore_wait(barrier, 3))
+    pl.when(top)(lambda: pl.semaphore_wait(barrier, 1))
 
     def rows_of(c):
         return pl.ds(pl.multiple_of(c * cut, cut), cut)
 
-    def copy_of(d, c):
-        return pltpu.make_async_remote_copy(
-            src_ref=(own if d == 2 and isinstance(c, int) and c == 0 else a_ref).at[:, rows_of(c), :],
+    def copy_of(d, c, held=False):
+        return pltpu.make_async_remote_copy(
+            src_ref=(own if held else a_ref).at[:, rows_of(c), :],
             dst_ref=partner.at[d, c],
             send_sem=send_sem.at[d],
             recv_sem=recv_sem.at[d, c],
@@ -107,19 +119,50 @@
         else:
             pl.when(condition)(act)
 
-    load(0).wait()
-    for c in range(last):
+    def begin():
+        load(0).wait()
+        copy_of(2, 0, True).start()
+
+    pl.when(lower)(begin)
+    pl.when(top)(lambda: copy_of(2, 0).start())
+    for c in range(1, last):
         copy_of(2, c).start()
     tail_copy(0).start()
-    for c in range(chunks):
-        when(yields, lambda: copy_of(0, c).start())
-        copy_of(1, c).start()
+    def across():
+        for c in range(chunks):
+            when(yields, lambda: copy_of(0, c).start())
+            copy_of(1, c).start()
+
+    def pass_on(d):
+        for turn_no in range(sizes[d] - 1):
+            pl.semaphore_signal(
+                token.at[d], inc=1, device_id=beside(d, plan.toward[d]), device_id_type=MESH
+            )
+            pl.semaphore_wait(token.at[d], 1)
+
+    def spread():
+        across()
+        pass_on(1)
+        pass_on(0)
+
+    def relay():
+        pl.semaphore_signal(token.at[3], inc=1, device_id=beside(2, 1), device_id_type=MESH)
+
+    pl.when(lower)(spread)
+    pl.when(below)(relay)
+
+    def follow():
+        pl.semaphore_wait(token.at[3], 1)
+        across()
+
+    pl.when(top)(follow)
 
     total[...] = jnp.zeros_like(total)
     diag_re[...] = jnp.zeros_like(diag_re)
     diag_im[...] = jnp.zeros_like(diag_im)
     rows[...] = jnp.zeros_like(rows)
     shifts.wait()
+    pl.when(top)(lambda: load(0).wait())
     load(1).wait()
     for d in range(3):
         if d == 0 and plan.paired:
@@ -142,12 +185,7 @@
 
         lax.fori_loop(0, bands // STRIP, turn, 0)
 
-    for d in (1, 0, 2):
-        for turn_no in range(sizes[d] - 1):
-            pl.semaphore_signal(
-                token.at[d], inc=1, device_id=beside(d, plan.toward[d]), device_id_type=MESH
-            )
-            pl.semaphore_wait(token.at[d], 1)
+    pass_on(2)
 
     row = lax.broadcasted_iota(jnp.int32, (ROWS, cut), 0)
     column = lax.broadcasted_iota(jnp.int32, (ROWS, cut), 1)
@@ -434,7 +472,7 @@
                 dma((4,)),
                 dma((6,)),
                 dma((2,)),
-                pltpu.SemaphoreType.REGULAR((3,)),
+                pltpu.SemaphoreType.REGULAR((4,)),
             ],
             compiler_params=pltpu.CompilerParams(
                 collective_id=0, has_side_effects=True, vmem_limit_bytes=60 * 1024 * 1024

time: 103 us -> 103 us (level)
  no operation moved by 1% of the time
where the time goes in v6:
time: 103 us
  Pallas kernels  102 us (99%)
    pallas_call x1, Pallas kernels, shards(): pl.pallas_call(functools.partial(kernel, plan), out_shape=tuple((pltpu.VM...  102 us

profile of v6, /device:TPU:0, one launch (start us, length us, event | category | flops | bytes accessed | tf_op | source)
XLA Modules:
  0.0 103.0 jit_solution(16617483510797730381)
XLA Ops:
  0.6 101.8 %shard_map.49 = (f32[3,512]{1,0:T(4,128)S(1)}, f32[3,512]{1,0:T(4,128)S(1)}, f32[1,3]{1,0:T(1,128)S(1)}) custom-call(s32[3]{0:T(128)} %shift_hbm.1, bf16[2,512,2048]{2,1,0:T(8,128)(2,1)} %bitcast.2), custom_call_target="tpu_custom_call" | custom-call | tf_op jit(solution)/shard_map/pallas_call | solution.py:447
  102.4 0.6 shard_map.50
